TPU v7x, 256 devices: a whole 4x4x8 slice. The times are simulated.
256 devices in a mesh: shard: 32 (over y, x, core), dp: 8 (over z).
Axes of the slice: x: 4, y: 4, z: 8, core: 2. Of those that a mesh axis runs over, the one named last changes fastest.
Arguments:
- grad: float32 [288, 128, 4096], P('shard', 'dp'), may hold values from -252 to 252
- param: bfloat16 [288, 128, 4096], P('shard', 'dp'), may hold values from -0.119628906 to 0.119628906
- row_state: float32 [288, 128], P('shard', 'dp'), may hold values from 0.3 to 27
- col_state: float32 [3, 4096], replicated, may hold values from 0.002 to 400
- block_start: int32 [32], replicated, may hold values from 0 to 143, as said below
- block_matrix: int32 [144], replicated, may hold values from 0 to 2, as said below
- step: int32 [1], replicated, may hold values from 2 to 11
Outputs:
- new_params: bfloat16 [18432, 4096], P(None, 'shard')
- new_row_state: float32 [288, 128], P('shard', 'dp')
- new_col_state: float32 [3, 4096], replicated
Inputs may be any that keep to these rules, and one draw needn't show every extreme that they name: block_start rises from 0 at index 0; every shard index owns between 1 and 9 consecutive global blocks, held in its first slots, and some index owns exactly 9; slots past a device's owned count hold values that no output reads. `block_matrix`: ids 0 and 1 each label 4096 / 128 blocks and id 2 labels 10240 / 128 blocks, in any order.
All inputs are finite; a program needn't handle non-finite values.
Results may differ from a plain program's by a relative error of at most 0.0004.
Values may be sent and summed in bfloat16 or wider, within the bound.
A program may use at most 64 MiB of HBM per device.

v0:
```python
import jax
import jax.numpy as jnp
from jax import lax
from jax.sharding import Mesh
from jax.sharding import PartitionSpec as P

D = 4096
FF = 10240
SHARD = ("shard_0", "shard_1", "shard_2")


def cut_along(shard, dim, length):
    shape = shard.shape
    blocks = shard.reshape(*shape[:dim], length, shape[dim] // length, *shape[dim + 1 :])
    return jnp.moveaxis(blocks, dim, 0)


def summed_on_arrival(shard, axis, dim):
    length = lax.axis_size(axis)
    blocks = lax.all_to_all(cut_along(shard, dim, length), axis, 0, 0, tiled=True)
    return jnp.sum(blocks, axis=0)


def summed_rows(shard, axes, dim):
    far, near = axes
    blocks = cut_along(shard, dim, lax.axis_size(far))
    nearer = summed_on_arrival(blocks, near, dim + 1)
    arrived = lax.all_to_all(nearer, far, split_axis=0, concat_axis=0, tiled=True)
    return arrived.sum(axis=0)


def filled_up(lines, length):
    spare = -lines.shape[0] % length
    if not spare:
        return lines
    return jnp.concatenate([lines, jnp.zeros((spare, *lines.shape[1:]), lines.dtype)])


def sent_to_all(shard, axis):
    copies = jnp.broadcast_to(shard, (lax.axis_size(axis), *shard.shape))
    return lax.all_to_all(copies, axis, split_axis=0, concat_axis=0, tiled=True)


def in_order(blocks, dim):
    shape = list(blocks.shape[1:])
    shape[dim] *= blocks.shape[0]
    return jnp.moveaxis(blocks, 0, dim).reshape(shape)


def whole_of(shard, axes, dim):
    far, near = axes
    blocks = sent_to_all(sent_to_all(shard, far), near)
    return in_order(blocks.swapaxes(0, 1).reshape(-1, *shard.shape), dim)


def sum_by_parts(shard, axes):
    own = summed_rows(filled_up(shard, lax.axis_size(axes[0]) * lax.axis_size(axes[1])), axes, 0)
    whole = whole_of(own, axes, 0)
    return whole[: len(shard)].reshape(shard.shape)


def together(arrays, axis):
    ravelled, at, gathered = (jnp.concatenate([a.reshape(-1) for a in arrays]), 0, [])
    subtotal = sum_by_parts(ravelled, axis)
    for a in arrays:
        gathered.append(subtotal[at : at + a.size].reshape(a.shape))
        at += a.size
    return tuple(gathered)


def moved_by_axis(blocks, axes, turns):
    shape = [lax.axis_size(a) for a in axes]
    blocks = blocks.reshape(*shape, *blocks.shape[1:])
    for k in turns:
        blocks = lax.all_to_all(blocks, axes[k], split_axis=k, concat_axis=k, tiled=True)
    return blocks.reshape(-1, *blocks.shape[len(axes) :])


def exchange_by_chip(shard, groups, turns, split_dim, concat_dim):
    length = lax.axis_size(groups[0]) * lax.axis_size(groups[1])
    blocks = cut_along(shard, split_dim, length)
    return in_order(moved_by_axis(blocks, groups, turns), concat_dim)


def scale_grad(grad, safe_rows, matrix_pick, new_cols, row_avg):
    slot_cols = jnp.dot(matrix_pick, new_cols, precision=lax.Precision.HIGHEST)
    slot_avg = jnp.dot(matrix_pick, row_avg, precision=lax.Precision.HIGHEST)
    return grad / jnp.sqrt(safe_rows[:, :, None] * slot_cols[:, None, :] / slot_avg[:, None, None])


def body(grad, param, row_state, col_state, block_start, block_matrix, step):
    slot_count = grad.shape[0]
    total_blocks = block_matrix.shape[0]
    shard_index = lax.axis_index(SHARD)
    block_ends = jnp.concatenate([block_start[1:], jnp.full((1,), total_blocks, jnp.int32)])
    first_block = lax.dynamic_index_in_dim(block_start, shard_index, keepdims=False)
    owned_count = lax.dynamic_index_in_dim(block_ends, shard_index, keepdims=False) - first_block
    slot_ids = jnp.arange(slot_count, dtype=jnp.int32)
    live_slot = slot_ids < owned_count
    block_ids = first_block + slot_ids
    block_table = block_ids[:, None] == jnp.arange(total_blocks, dtype=jnp.int32)[None, :]
    matrix_ids = jnp.sum(jnp.where(block_table, block_matrix[None, :], 0), axis=1)
    matrix_ids = jnp.where(live_slot, matrix_ids, 0)
    matrix_pick = (matrix_ids[:, None] == jnp.arange(3, dtype=jnp.int32)[None, :]).astype(
        jnp.float32
    )
    member = matrix_pick * live_slot[:, None].astype(jnp.float32)
    row_count = jnp.array([D, D, FF], jnp.float32)
    step_value = step[0].astype(jnp.float32)
    decay_rate = 1.0 - step_value ** (-0.8)
    learn_rate = 1.0 / jnp.sqrt(jnp.maximum(step_value, 10000.0))
    squares = grad * grad
    new_rows = jnp.where(
        live_slot[:, None],
        decay_rate * row_state + (1.0 - decay_rate) * jnp.sum(squares, axis=2) / D,
        0.0,
    )
    safe_rows = jnp.where(live_slot[:, None], new_rows, 1.0)
    col_part = jnp.einsum(
        "sm,sd->md", member, jnp.sum(squares, axis=1), precision=lax.Precision.HIGHEST
    )
    row_part = jnp.dot(jnp.sum(new_rows, axis=1), member, precision=lax.Precision.HIGHEST)
    quot_part = jnp.einsum(
        "sm,sd->md",
        member,
        jnp.sum(squares / safe_rows[:, :, None], axis=1),
        precision=lax.Precision.HIGHEST,
    )
    col_total, quot_total, row_total = together(
        (col_part, quot_part, row_part), (("shard_0", "shard_1"), ("shard_2", "dp"))
    )
    new_cols = decay_rate * col_state + (1.0 - decay_rate) * col_total / row_count[:, None]
    row_avg = row_total / row_count
    scaled = scale_grad(grad, safe_rows, matrix_pick, new_cols, row_avg)
    square_total = row_avg * jnp.sum(quot_total / new_cols, axis=1)
    clip_factor = jnp.maximum(1.0, jnp.sqrt(square_total / (row_count * D)))
    slot_clip = jnp.dot(matrix_pick, clip_factor, precision=lax.Precision.HIGHEST)
    updated = jnp.where(
        live_slot[:, None, None],
        param.astype(jnp.float32) - learn_rate * scaled / slot_clip[:, None, None],
        0.0,
    ).astype(jnp.bfloat16)
    column_rows = exchange_by_chip(updated, (("shard_0", "shard_1"), "shard_2"), (1, 0), 2, 0)
    spread = lax.all_gather(column_rows, "dp", axis=1, tiled=True)
    block_index = jnp.arange(total_blocks, dtype=jnp.int32)
    block_owner = (
        jnp.sum((block_start[None, :] <= block_index[:, None]).astype(jnp.int32), axis=1) - 1
    )
    slot_of = block_owner * slot_count + block_index - jnp.take(block_start, block_owner)
    new_params = jnp.take(spread, slot_of, axis=0).reshape(
        total_blocks * spread.shape[1], spread.shape[2]
    )
    return (new_params, new_rows, new_cols)


def solution(mesh):
    finer = Mesh(
        mesh.devices.reshape(4, 4, 2, mesh.shape["dp"]), ("shard_0", "shard_1", "shard_2", "dp")
    )
    in_specs = (P(SHARD, "dp", None), P(SHARD, "dp", None), P(SHARD, "dp"), P(), P(), P(), P())
    out_specs = (P(None, SHARD), P(SHARD, "dp"), P())
    return jax.shard_map(body, mesh=finer, in_specs=in_specs, out_specs=out_specs, check_vma=False)
```

profile of v0, /device:TPU:2, one launch (start us, length us, event | category | flops | bytes accessed | tf_op | source)
XLA Modules:
  0.0 263.2 jit_solution(12649364172545486583)
XLA Ops:
  7.2 0.9 slice.16
  8.1 1.2 dynamic_slice.8
  9.3 0.1 pad_add_fusion
  9.4 0.6 dynamic_slice.7
  10.0 1.2 iota_add_fusion
  13.1 1.9 multiply_reduce_fusion.1
  15.1 0.8 fusion.32
  15.9 0.1 broadcast_select_fusion
  15.9 0.5 copy-done.4
  16.5 1.6 divide_reduce_fusion
  18.1 0.9 select_reduce_fusion
  19.0 1.0 fusion.1
  20.1 1.5 reshape.144
  21.5 2.0 fusion.3
  23.5 1.5 reshape.143
  25.0 1.4 convolution_bitcast_fusion.2
  26.4 1.5 concatenate.7
  27.9 1.8 reshape_reshape.9
  29.7 0.9 copy.23
  30.7 17.0 %all_to_all.38 = f32[16,16,97]{2,1,0:T(8,128)} all-to-all(f32[16,16,97]{2,1,0:T(8,128)S(1)} %copy.23), channel_id=1, replica_groups=mesh['shard_0'=4,'shard_1'=4,'shard_2'=2,'dp'=8] {'shard_2','dp'}, dimensions={0} | all-to-all | bytes 198656 | tf_op jit(solution)/shard_map/all_to_all | solution.py:20
  47.7 0.9 reduce_sum.87
  48.6 13.6 %all_to_all.39 = f32[16,1,97]{2,1,0:T(1,128)} all-to-all(f32[16,1,97]{2,1,0:T(1,128)S(1)} %bitcast.48), channel_id=1, replica_groups=mesh['shard_0'=4,'shard_1'=4,'shard_2'=2,'dp'=8] {'shard_0','shard_1'}, dimensions={0} | all-to-all | bytes 12416 | tf_op jit(solution)/shard_map/all_to_all | solution.py:28
  62.2 0.7 reduce_sum.88
  63.0 10.6 %all_to_all.40 = f32[16,1,97]{2,1,0:T(1,128)S(1)} all-to-all(f32[16,1,97]{2,1,0:T(1,128)S(1)} %broadcast_in_dim.106), channel_id=1, replica_groups=mesh['shard_0'=4,'shard_1'=4,'shard_2'=2,'dp'=8] {'shard_0','shard_1'}, dimensions={0} | all-to-all | bytes 12416 | tf_op jit(solution)/shard_map/all_to_all | solution.py:41
  73.5 0.7 broadcast_in_dim.107
  74.2 4.2 %all-to-all-start.3 = ((f32[16,16,97]{2,1,0:T(8,128)}), f32[16,16,97]{2,1,0:T(8,128)}, u32[]{:S(2)}, u32[]{:S(2)}) async-start(f32[16,16,97]{2,1,0:T(8,128)} %broadcast_in_dim.107), calls=%async_computation.3 | async-start | bytes 262144 | tf_op jit(solution)/shard_map/all_to_all | solution.py:41
  78.5 8.4 %all-to-all-done.3 = f32[16,16,97]{2,1,0:T(8,128)} async-done(((f32[16,16,97]{2,1,0:T(8,128)}), f32[16,16,97]{2,1,0:T(8,128)}, u32[]{:S(2)}, u32[]{:S(2)}) %all-to-all-start.3) | async-done | bytes 99360 | tf_op jit(solution)/shard_map/all_to_all | solution.py:41
  86.8 1.6 copy.24
  88.4 1.7 reshape_reshape.10
  90.2 1.5 slice_multiply_fusion
  91.6 1.4 mul.105
  93.1 1.4 reshape.145
  94.5 0.9 convolution_bitcast_fusion.1
  95.4 1.2 divide_reduce_fusion.1
  96.6 1.0 fusion.5
  97.6 0.9 convolution_bitcast_fusion
  98.5 1.6 select_convert_fusion
  100.1 0.2 copy.30
  100.4 0.5 copy.26
  100.8 4.7 %all_to_all.41 = bf16[16,2,9,16,128]{4,3,2,0,1:T(8,128)(2,1)S(1)} all-to-all(bf16[16,2,9,16,128]{4,3,2,0,1:T(8,128)(2,1)S(1)} %copy.26), channel_id=1, replica_groups=mesh['shard_0'=4,'shard_1'=4,'shard_2'=2,'dp'=8] {'shard_2'}, dimensions={1} | all-to-all | bytes 2359296 | tf_op jit(solution)/shard_map/all_to_all | solution.py:75
  105.5 0.2 copy.27
  105.7 22.5 %all_to_all.42 = bf16[16,2,9,16,128]{4,3,2,1,0:T(8,128)(2,1)} all-to-all(bf16[16,2,9,16,128]{4,3,2,1,0:T(8,128)(2,1)S(1)} %copy.27), channel_id=1, replica_groups=mesh['shard_0'=4,'shard_1'=4,'shard_2'=2,'dp'=8] {'shard_0','shard_1'}, dimensions={0} | all-to-all | bytes 2359296 | tf_op jit(solution)/shard_map/all_to_all | solution.py:75
  128.3 0.1 convert_reduce_fusion
  128.4 1.6 gather_fusion
  130.0 0.1 broadcast_bitcast_fusion
  130.1 101.9 %all-gather.2.cloned.1.call-done = bf16[288,128,128]{2,1,0:T(8,128)(2,1)} async-done(((bf16[288,16,128]{2,1,0:T(8,128)(2,1)}), bf16[288,128,128]{2,1,0:T(8,128)(2,1)}) %all-gather.2.cloned.1.call-update) | async-done | bytes 9437200 | tf_op jit(solution)/shard_map/all_gather | solution.py:144
  232.0 11.3 %gather_fusion.1 = bf16[144,128,128]{2,1,0:T(8,128)(2,1)} fusion(bf16[288,128,128]{2,1,0:T(8,128)(2,1)} %all-gather.2.cloned.1.call-done, s32[1024]{0:T(1024)S(1)} %pad_clamp_fusion), kind=kCustom, calls=%fused_computation.1 | custom fusion | bytes 9437760 | tf_op jit(solution)/shard_map/jit(_take)/gather | solution.py:150
  243.3 13.0 %bitcast_select_fusion = bf16[18432,128]{1,0:T(8,128)(2,1)} fusion(bf16[144,128,128]{2,1,0:T(8,128)(2,1)} %gather_fusion.1, pred[18432]{0:T(1024)(128)(4,1)S(1)} %broadcast_bitcast_fusion), kind=kLoop, calls=%fused_computation.2 | loop fusion | flops 2359296 | bytes 9455616 | tf_op jit(solution)/shard_map/jit(_take)/select_n | solution.py:150
  (29 shorter events, 0.2 us)
Async XLA Ops:
  7.2 9.3 %copy-start.1 = (f32[9,16,4096]{2,1,0:T(8,128)S(1)}, f32[9,16,4096]{2,1,0:T(8,128)}, u32[]{:S(2)}) copy-start(f32[9,16,4096]{2,1,0:T(8,128)} %param.8) | copy-start | bytes 7077892
  7.2 7.9 %copy-start.5 = (f32[9,16]{1,0:T(8,128)S(1)}, f32[9,16]{1,0:T(8,128)}, u32[]{:S(2)}) copy-start(f32[9,16]{1,0:T(8,128)} %param.10) | copy-start | bytes 1732
  12.4 3.5 %copy-start.7 = (pred[9]{0:T(512)(128)(4,1)}, pred[9]{0:T(512)(128)(4,1)S(1)}, u32[]{:S(2)}) copy-start(pred[9]{0:T(512)(128)(4,1)S(1)} %get-tuple-element.13) | copy-start | bytes 31
  13.1 5.0 %copy-start.8 = (s32[144]{0:T(256)S(1)}, s32[144]{0:T(256)}, u32[]{:S(2)}) copy-start(s32[144]{0:T(256)} %param.13) | copy-start | bytes 1732
  15.9 0.6 copy-start.4
  18.1 80.4 %copy-start.2 = (bf16[9,16,4096]{2,1,0:T(8,128)(2,1)S(1)}, bf16[9,16,4096]{2,1,0:T(8,128)(2,1)}, u32[]{:S(2)}) copy-start(bf16[9,16,4096]{2,1,0:T(8,128)(2,1)} %param.9) | copy-start | bytes 3538948
  19.0 11.6 %copy-start.6 = (s32[9]{0:T(128)}, s32[9]{0:T(128)S(1)}, u32[]{:S(2)}) copy-start(s32[9]{0:T(128)S(1)} %broadcast_select_fusion.1) | copy-start | bytes 112
  74.2 12.7 %all-to-all-start.3 = ((f32[16,16,97]{2,1,0:T(8,128)}), f32[16,16,97]{2,1,0:T(8,128)}, u32[]{:S(2)}, u32[]{:S(2)}) async-start(f32[16,16,97]{2,1,0:T(8,128)} %broadcast_in_dim.107), calls=%async_computation.3 | async-start | bytes 262144 | tf_op jit(solution)/shard_map/all_to_all | solution.py:41
  78.4 153.6 %all-gather.2.cloned.1.call-start = ((), (), s32[]{:S(2)}) async-start(), calls=%async_computation.6 | async-start | bytes 10616832 | tf_op jit(solution)/shard_map/all_gather | solution.py:144
  96.6 1.9 copy-start.3
  105.7 22.5 %copy-start = (s32[32]{0:T(128)S(1)}, s32[32]{0:T(128)}, u32[]{:S(2)}) copy-start(s32[32]{0:T(128)} %param.12) | copy-start | bytes 388
Sparse Core Ops, SparseCore 0:
  128.4 103.5 all-gather.1
where the time goes:
time: 265 us; the launch traced here: 263 us
  waiting for transfers between devices  110 us (42%)
  blocking collectives  68.3 us (26%)
  local copies, waits for them, and re-layouts  31.3 us (12%)
  other arithmetic  25.5 us (10%)
  between operations  16.3 us (6%)
  matrix products  7.16 us (3%)
  starting transfers between devices  4.21 us (2%)
    all_gather x1, waiting for transfers between devices, body(): spread = lax.all_gather(column_rows, 'dp', axis=1, tiled=True)  102 us
    all_to_all x2, blocking collectives, moved_by_axis(): lax.all_to_all(blocks, axes[k], split_axis=k, concat_axis=k, tiled=True)  27.2 us
    all_to_all x1, blocking collectives, summed_on_arrival(): lax.all_to_all(cut_along(shard, dim, length), axis, 0, 0, tiled=True)  17 us
    all_to_all x1, blocking collectives, summed_rows(): lax.all_to_all(nearer, far, split_axis=0, concat_axis=0, tiled=True)  13.6 us
    select_n x2, other arithmetic, body(): jnp.take(spread, slot_of, axis=0)  13 us
    gather x1, local copies, waits for them, and re-layouts, body(): jnp.take(spread, slot_of, axis=0)  11.3 us
    all_to_all x1, blocking collectives, sent_to_all(): return lax.all_to_all(copies, axis, split_axis=0, concat_axis=0, tiled=True)  10.6 us
    all_to_all x1, waiting for transfers between devices, sent_to_all(): return lax.all_to_all(copies, axis, split_axis=0, concat_axis=0, tiled=True)  8.38 us
  transfers between devices with their start and end apart: 2, of which 2 were waited for; matrix products, arithmetic and copies ran while one was open for 1% of the time, Pallas kernels for 0%

commit v1 on v0

--- a/solution.py
+++ b/solution.py
@@ -7,6 +7,9 @@
 D = 4096
 FF = 10240
 SHARD = ("shard_0", "shard_1", "shard_2")
+arrange_node = lambda x_in, axis_name: jnp.concatenate(
+    lax.all_to_all(jnp.stack([x_in for _ in range(lax.psum(1, axis_name))]), axis_name, 0, 0), 1
+)
 
 
 def cut_along(shard, dim, length):
@@ -141,7 +144,7 @@
         0.0,
     ).astype(jnp.bfloat16)
     column_rows = exchange_by_chip(updated, (("shard_0", "shard_1"), "shard_2"), (1, 0), 2, 0)
-    spread = lax.all_gather(column_rows, "dp", axis=1, tiled=True)
+    spread = arrange_node(column_rows, axis_name="dp")
     block_index = jnp.arange(total_blocks, dtype=jnp.int32)
     block_owner = (
         jnp.sum((block_start[None, :] <= block_index[:, None]).astype(jnp.int32), axis=1) - 1

time: 265 us -> 377 us (1.42)
  waiting for transfers between devices: 110 us -> 215 us
  local copies, waits for them, and re-layouts: 31.3 us -> 46.2 us
  between operations: 16.3 us -> 2.94 us
  starting transfers between devices: 4.21 us -> 9.51 us
    all_to_all x0 -> x1, waiting for transfers between devices: none -> 206 us  [lax.all_to_all(jnp.stack([x_in for _ in range(lax.psum(1, axis_name))]),...]
    all_gather x1 -> x0, waiting for transfers between devices: 102 us -> none  [body(): spread = lax.all_gather(column_rows, 'dp', axis=1, tiled=True)]
    all_to_all x0 -> x1, local copies, waits for them, and re-layouts: none -> 10.1 us  [lax.all_to_all(jnp.stack([x_in for _ in range(lax.psum(1, axis_name))]),...]
    all_to_all x0 -> x1, starting transfers between devices: none -> 5.34 us  [lax.all_to_all(jnp.stack([x_in for _ in range(lax.psum(1, axis_name))]),...]
    another operation x0 -> x1, local copies, waits for them, and re-layouts: none -> 4.87 us  [jnp.stack([x_in for _ in range(lax.psum(1, axis_name))])]
  transfers between devices with their start and end apart: 2 -> 2, of which waited for: 2 -> 2; matrix products, arithmetic and copies ran while one was open for 1% -> 0% of each run, Pallas kernels for 0% -> 0%
where the time goes in v1:
time: 377 us; the launch traced here: 374 us
  waiting for transfers between devices  215 us (57%)
  blocking collectives  67.7 us (18%)
  local copies, waits for them, and re-layouts  46.2 us (12%)
  other arithmetic  25.5 us (7%)
  starting transfers between devices  9.51 us (3%)
  matrix products  7.16 us (2%)
    all_to_all x1, waiting for transfers between devices, lax.all_to_all(jnp.stack([x_in for _ in range(lax.psum(1, axis_name))]),...  206 us
    all_to_all x2, blocking collectives, moved_by_axis(): lax.all_to_all(blocks, axes[k], split_axis=k, concat_axis=k, tiled=True)  26.5 us
    all_to_all x1, blocking collectives, summed_on_arrival(): lax.all_to_all(cut_along(shard, dim, length), axis, 0, 0, tiled=True)  17 us
    all_to_all x1, blocking collectives, summed_rows(): lax.all_to_all(nearer, far, split_axis=0, concat_axis=0, tiled=True)  13.6 us
    select_n x2, other arithmetic, body(): jnp.take(spread, slot_of, axis=0)  13 us
    gather x1, local copies, waits for them, and re-layouts, body(): jnp.take(spread, slot_of, axis=0)  11.2 us
    all_to_all x1, blocking collectives, sent_to_all(): return lax.all_to_all(copies, axis, split_axis=0, concat_axis=0, tiled=True)  10.6 us
    all_to_all x1, local copies, waits for them, and re-layouts, lax.all_to_all(jnp.stack([x_in for _ in range(lax.psum(1, axis_name))]),...  10.1 us
  transfers between devices with their start and end apart: 2, of which 2 were waited for; matrix products, arithmetic and copies ran while one was open for 0% of the time, Pallas kernels for 0%

profile of v1, /device:TPU:2, one launch (start us, length us, event | category | flops | bytes accessed | tf_op | source)
XLA Modules:
  0.0 373.7 jit_solution(1401741698100877678)
XLA Ops:
  0.7 0.9 slice.16
  1.5 1.2 dynamic_slice.8
  2.9 0.6 dynamic_slice.7
  3.4 1.2 iota_add_fusion
  6.6 1.9 multiply_reduce_fusion.1
  8.6 0.8 fusion.32
  9.4 0.5 copy-done.4
  9.9 1.6 divide_reduce_fusion
  11.5 0.9 select_reduce_fusion
  12.5 1.0 fusion.1
  13.5 1.5 reshape.152
  15.0 2.0 fusion.3
  17.0 1.5 reshape.151
  18.5 1.4 convolution_bitcast_fusion.2
  19.9 1.5 concatenate.7
  21.4 1.8 reshape_reshape.6
  23.2 0.9 copy.26
  24.1 17.0 %all_to_all.43 = f32[16,16,97]{2,1,0:T(8,128)} all-to-all(f32[16,16,97]{2,1,0:T(8,128)S(1)} %copy.26), channel_id=1, replica_groups=mesh['shard_0'=4,'shard_1'=4,'shard_2'=2,'dp'=8] {'shard_2','dp'}, dimensions={0} | all-to-all | bytes 198656 | tf_op jit(solution)/shard_map/all_to_all | solution.py:23
  41.2 0.9 reduce_sum.87
  42.1 13.6 %all_to_all.44 = f32[16,1,97]{2,1,0:T(1,128)} all-to-all(f32[16,1,97]{2,1,0:T(1,128)S(1)} %bitcast.52), channel_id=1, replica_groups=mesh['shard_0'=4,'shard_1'=4,'shard_2'=2,'dp'=8] {'shard_0','shard_1'}, dimensions={0} | all-to-all | bytes 12416 | tf_op jit(solution)/shard_map/all_to_all | solution.py:31
  55.7 0.7 reduce_sum.88
  56.4 10.6 %all_to_all.45 = f32[16,1,97]{2,1,0:T(1,128)S(1)} all-to-all(f32[16,1,97]{2,1,0:T(1,128)S(1)} %broadcast_in_dim.106), channel_id=1, replica_groups=mesh['shard_0'=4,'shard_1'=4,'shard_2'=2,'dp'=8] {'shard_0','shard_1'}, dimensions={0} | all-to-all | bytes 12416 | tf_op jit(solution)/shard_map/all_to_all | solution.py:44
  67.0 0.7 broadcast_in_dim.107
  67.7 4.2 %all-to-all-start.3 = ((f32[16,16,97]{2,1,0:T(8,128)}), f32[16,16,97]{2,1,0:T(8,128)}, u32[]{:S(2)}, u32[]{:S(2)}) async-start(f32[16,16,97]{2,1,0:T(8,128)} %broadcast_in_dim.107), calls=%async_computation.3 | async-start | bytes 262144 | tf_op jit(solution)/shard_map/all_to_all | solution.py:44
  71.9 8.4 %all-to-all-done.3 = f32[16,16,97]{2,1,0:T(8,128)} async-done(((f32[16,16,97]{2,1,0:T(8,128)}), f32[16,16,97]{2,1,0:T(8,128)}, u32[]{:S(2)}, u32[]{:S(2)}) %all-to-all-start.3) | async-done | bytes 99360 | tf_op jit(solution)/shard_map/all_to_all | solution.py:44
  80.3 1.6 copy.27
  81.9 1.7 reshape_reshape.7
  83.7 1.5 slice_multiply_fusion
  85.1 1.4 mul.105
  86.6 1.4 reshape.153
  88.0 0.9 convolution_bitcast_fusion.1
  88.9 1.2 divide_reduce_fusion.1
  90.1 1.0 fusion.5
  91.0 0.9 convolution_bitcast_fusion
  92.0 1.6 select_convert_fusion
  93.6 0.2 copy.34
  93.8 0.5 copy.29
  94.3 4.7 %all_to_all.46 = bf16[16,2,9,16,128]{4,3,2,0,1:T(8,128)(2,1)S(1)} all-to-all(bf16[16,2,9,16,128]{4,3,2,0,1:T(8,128)(2,1)S(1)} %copy.29), channel_id=1, replica_groups=mesh['shard_0'=4,'shard_1'=4,'shard_2'=2,'dp'=8] {'shard_2'}, dimensions={1} | all-to-all | bytes 2359296 | tf_op jit(solution)/shard_map/all_to_all | solution.py:78
  99.0 0.2 copy.30
  99.2 21.8 %all_to_all.47 = bf16[16,2,9,16,128]{4,3,2,1,0:T(8,128)(2,1)S(1)} all-to-all(bf16[16,2,9,16,128]{4,3,2,1,0:T(8,128)(2,1)S(1)} %copy.30), channel_id=1, replica_groups=mesh['shard_0'=4,'shard_1'=4,'shard_2'=2,'dp'=8] {'shard_0','shard_1'}, dimensions={0} | all-to-all | bytes 2359296 | tf_op jit(solution)/shard_map/all_to_all | solution.py:78
  121.0 4.9 %stack.3 = bf16[8,288,16,128]{3,2,1,0:T(8,128)(2,1)} broadcast(bf16[288,16,128]{2,1,0:T(8,128)(2,1)S(1)} %bitcast.50), dimensions={1,2,3} | broadcast | bytes 10616832 | tf_op jit(solution)/shard_map/stack | solution.py:11
  125.9 5.3 %all-to-all-start.6 = ((bf16[8,288,16,128]{3,2,1,0:T(8,128)(2,1)}), bf16[8,288,16,128]{3,2,1,0:T(8,128)(2,1)}, u32[]{:S(2)}, u32[]{:S(2)}) async-start(bf16[8,288,16,128]{3,2,1,0:T(8,128)(2,1)} %stack.3), calls=%async_computation.6 | async-start | bytes 18874368 | tf_op jit(solution)/shard_map/all_to_all | solution.py:11
  131.3 0.1 convert_reduce_fusion
  131.4 1.6 gather_fusion
  133.1 206.2 %all-to-all-done.6 = bf16[8,288,16,128]{3,2,1,0:T(8,128)(2,1)} async-done(((bf16[8,288,16,128]{3,2,1,0:T(8,128)(2,1)}), bf16[8,288,16,128]{3,2,1,0:T(8,128)(2,1)}, u32[]{:S(2)}, u32[]{:S(2)}) %all-to-all-start.6) | async-done | bytes 9437216 | tf_op jit(solution)/shard_map/all_to_all | solution.py:11
  339.3 10.1 %copy.31 = bf16[8,288,16,128]{3,2,0,1:T(8,128)(2,1)} copy(bf16[8,288,16,128]{3,2,1,0:T(8,128)(2,1)} %all-to-all-done.6) | data formatting | bytes 18874368 | tf_op jit(solution)/shard_map/all_to_all | solution.py:11
  349.5 11.2 %gather_fusion.1 = bf16[144,128,128]{2,1,0:T(8,128)(2,1)} fusion(bf16[288,128,128]{2,1,0:T(8,128)(2,1)} %bitcast.47, s32[1024]{0:T(1024)S(1)} %pad_clamp_fusion), kind=kCustom, calls=%fused_computation.1 | custom fusion | bytes 9437760 | tf_op jit(solution)/shard_map/jit(_take)/gather | solution.py:153
  360.7 13.0 %bitcast_select_fusion = bf16[18432,128]{1,0:T(8,128)(2,1)} fusion(bf16[144,128,128]{2,1,0:T(8,128)(2,1)} %gather_fusion.1, pred[18432]{0:T(1024)(128)(4,1)S(1)} %broadcast_bitcast_fusion), kind=kLoop, calls=%fused_computation.2 | loop fusion | flops 2359296 | bytes 9455616 | tf_op jit(solution)/shard_map/jit(_take)/select_n | solution.py:153
  (30 shorter events, 0.3 us)
Async XLA Ops:
  0.6 9.3 %copy-start.1 = (f32[9,16,4096]{2,1,0:T(8,128)S(1)}, f32[9,16,4096]{2,1,0:T(8,128)}, u32[]{:S(2)}) copy-start(f32[9,16,4096]{2,1,0:T(8,128)} %param.8) | copy-start | bytes 7077892
  0.6 7.9 %copy-start.5 = (f32[9,16]{1,0:T(8,128)S(1)}, f32[9,16]{1,0:T(8,128)}, u32[]{:S(2)}) copy-start(f32[9,16]{1,0:T(8,128)} %param.10) | copy-start | bytes 1732
  5.9 3.5 copy-start.7
  6.6 5.0 %copy-start.8 = (s32[144]{0:T(256)S(1)}, s32[144]{0:T(256)}, u32[]{:S(2)}) copy-start(s32[144]{0:T(256)} %param.13) | copy-start | bytes 1732
  9.3 0.6 copy-start.4
  11.5 80.4 %copy-start.2 = (bf16[9,16,4096]{2,1,0:T(8,128)(2,1)S(1)}, bf16[9,16,4096]{2,1,0:T(8,128)(2,1)}, u32[]{:S(2)}) copy-start(bf16[9,16,4096]{2,1,0:T(8,128)(2,1)} %param.9) | copy-start | bytes 3538948
  12.5 11.7 %copy-start.6 = (s32[9]{0:T(128)}, s32[9]{0:T(128)S(1)}, u32[]{:S(2)}) copy-start(s32[9]{0:T(128)S(1)} %broadcast_select_fusion.1) | copy-start | bytes 112
  67.7 12.7 %all-to-all-start.3 = ((f32[16,16,97]{2,1,0:T(8,128)}), f32[16,16,97]{2,1,0:T(8,128)}, u32[]{:S(2)}, u32[]{:S(2)}) async-start(f32[16,16,97]{2,1,0:T(8,128)} %broadcast_in_dim.107), calls=%async_computation.3 | async-start | bytes 262144 | tf_op jit(solution)/shard_map/all_to_all | solution.py:44
  90.1 1.9 copy-start.3
  125.9 5.4 %copy-start = (s32[32]{0:T(128)S(1)}, s32[32]{0:T(128)}, u32[]{:S(2)}) copy-start(s32[32]{0:T(128)} %param.12) | copy-start | bytes 388
  125.9 213.4 %all-to-all-start.6 = ((bf16[8,288,16,128]{3,2,1,0:T(8,128)(2,1)}), bf16[8,288,16,128]{3,2,1,0:T(8,128)(2,1)}, u32[]{:S(2)}, u32[]{:S(2)}) async-start(bf16[8,288,16,128]{3,2,1,0:T(8,128)(2,1)} %stack.3), calls=%async_computation.6 | async-start | bytes 18874368 | tf_op jit(solution)/shard_map/all_to_all | solution.py:11
